TPU v7x, 32 devices: a whole 2x2x4 slice. The times are simulated.
32 devices in a mesh: clips: 2 (over x), seq: 16 (over z, y, core).
Axes of the slice: x: 2, y: 2, z: 4, core: 2. Of those that a mesh axis runs over, the one named last changes fastest.
Arguments:
- video_q: bfloat16 [4096, 1536], P(('clips', 'seq')), parts along dimension 0, may hold values from -200 to 200
- video_k: bfloat16 [4096, 1536], P(('clips', 'seq')), parts along dimension 0, may hold values from -7 to 7
- video_v: bfloat16 [4096, 1536], P(('clips', 'seq')), parts along dimension 0, may hold values from -6 to 6
- audio_q: bfloat16 [256, 1536], P(('clips', 'seq')), parts along dimension 0, may hold values from -200 to 200
- audio_k: bfloat16 [256, 1536], P(('clips', 'seq')), parts along dimension 0, may hold values from -6 to 6
- audio_v: bfloat16 [256, 1536], P(('clips', 'seq')), parts along dimension 0, may hold values from -6 to 6
- radius: int32 [32], P(('clips', 'seq')), parts along dimension 0, may hold values from 1 to 2
- tile_list: int32 [32, 5], P('clips'), parts along dimension 0, may hold values from -1 to 15, as said below
- tile_count: int32 [32], P('clips'), parts along dimension 0, may hold values from 1 to 5, as said below
- video_gain: float32 [1536], replicated, may hold values from 0.5 to 1.5
- audio_gain: float32 [1536], replicated, may hold values from 0.5 to 1.5
Outputs:
- video_out: bfloat16 [4096, 1536], P(('clips', 'seq')), parts along dimension 0
- audio_out: bfloat16 [256, 1536], P(('clips', 'seq')), parts along dimension 0
There are 2 independent parts, one for each index of `clips`. A program takes and returns all parts, laid end to end along the dimension named above; an argument that names none is the same for every part. Nothing has to cross between parts.
Inputs may be any that keep to these rules, and one draw needn't show every extreme that they name: `tile_list`: row b names tile b first, then tile_count[b] - 1 distinct other tiles within 4 of b; the remaining entries are -1. `tile_count`: some block lists 5 tiles.
All inputs are finite; a program needn't handle non-finite values.
Results may differ from a plain program's by a relative error of at most 0.014.
Values may be sent and summed in bfloat16 or wider, within the bound.
A program may use at most 64 MiB of HBM per device.

v0:
```python
import jax
import jax.numpy as jnp
from jax import lax
from jax.sharding import PartitionSpec as P

H = 12
HD = 128
RMAX = 2
SPAN = 4


negative_big = -1e30
epsilon = 1e-06
key_stride = 512


def passed_along(value, axis, steps):
    count = lax.axis_size(axis)
    first, last = (max(0, -steps), min(count, count - steps))
    return lax.ppermute(value, axis, [(source, source + steps) for source in range(first, last)])


def split_heads(matrix):
    return matrix.reshape(matrix.shape[0], H, HD)


def empty_state(row_count):
    return (
        jnp.full((H, row_count), negative_big, jnp.float32),
        jnp.zeros((H, row_count), jnp.float32),
        jnp.zeros((H, row_count, HD), jnp.float32),
    )


def attend_block(running, queries, key_block, value_block, allowed):
    old_peak, weight_sum, weighted = running
    scores = jnp.einsum(
        "qhd,khd->hqk",
        split_heads(queries),
        split_heads(key_block),
        preferred_element_type=jnp.float32,
    ) * HD ** (-0.5)
    scores = jnp.where(allowed, scores, negative_big)
    row_peak = jnp.maximum(old_peak, jnp.max(scores, axis=-1))
    shrink = jnp.exp(old_peak - row_peak)
    weights = jnp.exp(scores - row_peak[..., None]).astype(jnp.bfloat16)
    weight_sum = weight_sum * shrink + jnp.sum(weights.astype(jnp.float32), axis=-1)
    weighted = weighted * shrink[..., None] + jnp.einsum(
        "hqk,khd->hqd", weights, split_heads(value_block), preferred_element_type=jnp.float32
    )
    return (row_peak, weight_sum, weighted)


def attend_rows(running, queries, key_rows, value_rows, allowed):
    for row_start in range(0, key_rows.shape[0], key_stride):
        running = attend_block(
            running,
            queries,
            key_rows[row_start : row_start + key_stride],
            value_rows[row_start : row_start + key_stride],
            allowed,
        )
    return running


def finish(weight_sum, weighted, gain):
    mixed = weighted / weight_sum[..., None]
    mixed = jnp.transpose(mixed, (1, 0, 2)).reshape(mixed.shape[1], H * HD)
    mean_square = jnp.mean(mixed * mixed, axis=-1, keepdims=True)
    return (mixed * lax.rsqrt(mean_square + epsilon) * gain).astype(jnp.bfloat16)


def on_device(
    video_q,
    video_k,
    video_v,
    audio_q,
    audio_k,
    audio_v,
    radius,
    tile_list,
    tile_count,
    video_gain,
    audio_gain,
):
    tile_total = lax.axis_size("seq")
    my_tile = lax.axis_index("seq")
    query_rows = video_q.shape[0]
    audio_rows = audio_q.shape[0]
    nearby = {}
    for distance in range(1, RMAX + 1):
        for direction in (1, -1):
            nearby[direction * distance] = passed_along(
                (video_k, video_v), "seq", -direction * distance
            )
    video_state = attend_rows(empty_state(query_rows), video_q, video_k, video_v, True)
    my_radius = radius[0]
    for offset in sorted(nearby):
        far_keys, far_values = nearby[offset]
        inside = (
            (abs(offset) <= my_radius) & (my_tile + offset >= 0) & (my_tile + offset < tile_total)
        )
        video_state = attend_rows(video_state, video_q, far_keys, far_values, inside)
    video_state = attend_rows(
        video_state,
        video_q,
        lax.all_gather(audio_k, "seq", axis=0, tiled=True),
        lax.all_gather(audio_v, "seq", axis=0, tiled=True),
        True,
    )
    video_out = finish(video_state[1], video_state[2], video_gain)
    entry_live = jnp.arange(tile_list.shape[1], dtype=jnp.int32)[None, :] < tile_count[:, None]
    for distance in range(RMAX + 1, SPAN + 1):
        for direction in (1, -1):
            nearby[direction * distance] = passed_along(
                (video_k, video_v), "seq", -direction * distance
            )
    my_list = tile_list[my_tile]
    my_live = entry_live[my_tile]
    audio_state = attend_rows(empty_state(audio_rows), audio_q, video_k, video_v, True)
    for offset in sorted(nearby):
        far_keys, far_values = nearby[offset]
        is_listed = jnp.any((my_list == my_tile + offset) & my_live)
        audio_state = attend_rows(audio_state, audio_q, far_keys, far_values, is_listed)
    audio_out = finish(audio_state[1], audio_state[2], audio_gain)
    return (video_out, audio_out)


def solution(mesh):
    return jax.shard_map(
        on_device,
        mesh=mesh,
        in_specs=(
            P(("clips", "seq"), None),
            P(("clips", "seq"), None),
            P(("clips", "seq"), None),
            P(("clips", "seq"), None),
            P(("clips", "seq"), None),
            P(("clips", "seq"), None),
            P(("clips", "seq")),
            P("clips", None),
            P("clips"),
            P(),
            P(),
        ),
        out_specs=(P(("clips", "seq"), None), P(("clips", "seq"), None)),
        check_vma=False,
    )
```

profile of v0, /device:TPU:1, one launch (start us, length us, event | category | flops | bytes accessed | tf_op | source)
XLA Modules:
  0.0 156.3 jit_solution(11972619183756843965)
XLA Ops:
  0.6 1.2 copy.98
  1.9 4.0 %collective-permute-start = (bf16[128,1536]{0,1:T(8,128)(2,1)S(1)}, bf16[128,1536]{0,1:T(8,128)(2,1)S(1)}, u32[]{:S(2)}, u32[]{:S(2)}) collective-permute-start(bf16[128,1536]{0,1:T(8,128)(2,1)S(1)} %copy.98), channel_id=1, source_target_pairs={{0,2},{1,3},{2,4},{3,5},{4,6},{5,7},{6,8},{7,9},{8,10},{9,11},{10,... | collective-permute-start | bytes 1179656 | tf_op jit(solution)/shard_map/ppermute | solution.py:20
  5.9 1.3 collective-permute-start.6
  7.2 2.9 %collective-permute-start.4 = (bf16[128,1536]{0,1:T(8,128)(2,1)S(1)}, bf16[128,1536]{0,1:T(8,128)(2,1)S(1)}, u32[]{:S(2)}, u32[]{:S(2)}) collective-permute-start(bf16[128,1536]{0,1:T(8,128)(2,1)S(1)} %copy.98), channel_id=1, source_target_pairs={{1,0},{2,1},{3,2},{4,3},{5,4},{6,5},{7,6},{8,7},{9,8},{10,9},{11,1... | collective-permute-start | bytes 1179656 | tf_op jit(solution)/shard_map/ppermute | solution.py:20
  10.0 4.2 %collective-permute-start.2 = (bf16[128,1536]{0,1:T(8,128)(2,1)S(1)}, bf16[128,1536]{0,1:T(8,128)(2,1)S(1)}, u32[]{:S(2)}, u32[]{:S(2)}) collective-permute-start(bf16[128,1536]{0,1:T(8,128)(2,1)S(1)} %copy.98), channel_id=1, source_target_pairs={{0,1},{1,2},{2,3},{3,4},{4,5},{5,6},{6,7},{7,8},{8,9},{9,10},{10,1... | collective-permute-start | bytes 1179656 | tf_op jit(solution)/shard_map/ppermute | solution.py:20
  14.2 4.2 %collective-permute-start.8 = (bf16[128,1536]{0,1:T(8,128)(2,1)S(1)}, bf16[128,1536]{0,1:T(8,128)(2,1)}, u32[]{:S(2)}, u32[]{:S(2)}) collective-permute-start(bf16[128,1536]{0,1:T(8,128)(2,1)S(1)} %copy.98), channel_id=1, source_target_pairs={{0,4},{1,5},{2,6},{3,7},{4,8},{5,9},{6,10},{7,11},{8,12},{9,13},{1... | collective-permute-start | bytes 1179656 | tf_op jit(solution)/shard_map/ppermute | solution.py:20
  18.4 0.7 copy-done.62
  19.1 2.0 %copy.101 = bf16[128,1536]{0,1:T(8,128)(2,1)} copy(bf16[128,1536]{1,0:T(8,128)(2,1)} %param.13) | data formatting | bytes 786432 | tf_op args[2]
  22.0 0.5 copy-done.49
  22.5 23.8 %all_gather.6 = bf16[128,1536]{1,0:T(8,128)(2,1)S(1)} all-gather(bf16[8,1536]{1,0:T(8,128)(2,1)S(1)} %copy-done.49), channel_id=1, replica_groups=mesh['clips'=2,'seq'=16] {'seq'}, dimensions={0}, use_global_device_ids=true | all-gather | bytes 417792 | tf_op jit(solution)/shard_map/all_gather | solution.py:107
  46.4 0.5 copy-done.50
  47.0 21.8 %all_gather.7 = bf16[128,1536]{1,0:T(8,128)(2,1)S(1)} all-gather(bf16[8,1536]{1,0:T(8,128)(2,1)S(1)} %copy-done.50), channel_id=1, replica_groups=mesh['clips'=2,'seq'=16] {'seq'}, dimensions={0}, use_global_device_ids=true | all-gather | bytes 417792 | tf_op jit(solution)/shard_map/all_gather | solution.py:108
  68.8 0.9 copy.126
  70.4 0.8 and_reduce_fusion.1
  71.3 1.2 fusion.82
  72.7 1.3 collective-permute-start.14
  74.0 0.9 fusion.93
  75.0 1.3 collective-permute-start.12
  76.3 1.9 %fusion.90 = (f32[12,8]{1,0:T(8,128)S(1)}, f32[12,8,128]{2,1,0:T(8,128)S(1)}) fusion(bf16[128,12,128]{0,2,1:T(8,128)(2,1)} %bitcast.19, bf16[8,1536]{1,0:T(8,128)(2,1)S(1)} %copy-done, pred[]{:T(512)} %get-tuple-element.7), kind=kOutput, calls=%fused_computation.205 | convolution fusion | flops 3182496 | bytes 467329 | tf_op jit(solution)/shard_map/qhd,khd->hqk/dot_general | solution.py:37
  78.2 5.0 %collective-permute-start.10 = (bf16[128,1536]{0,1:T(8,128)(2,1)S(1)}, bf16[128,1536]{0,1:T(8,128)(2,1)S(1)}, u32[]{:S(2)}, u32[]{:S(2)}) collective-permute-start(bf16[128,1536]{0,1:T(8,128)(2,1)S(1)} %copy.98), channel_id=1, source_target_pairs={{0,3},{1,4},{2,5},{3,6},{4,7},{5,8},{6,9},{7,10},{8,11},{9,12},{10... | collective-permute-start | bytes 1179656 | tf_op jit(solution)/shard_map/ppermute | solution.py:20
  83.2 0.9 fusion.91
  84.1 1.3 collective-permute-start.1
  85.4 1.0 fusion.92
  86.4 5.0 %collective-permute-start.11 = (bf16[128,1536]{0,1:T(8,128)(2,1)}, bf16[128,1536]{0,1:T(8,128)(2,1)}, u32[]{:S(2)}, u32[]{:S(2)}) collective-permute-start(bf16[128,1536]{0,1:T(8,128)(2,1)} %copy.101), channel_id=1, source_target_pairs={{0,3},{1,4},{2,5},{3,6},{4,7},{5,8},{6,9},{7,10},{8,11},{9,12},{10... | collective-permute-start | bytes 1179656 | tf_op jit(solution)/shard_map/ppermute | solution.py:20
  91.4 2.4 %fusion.95 = (f32[12,8]{1,0:T(8,128)S(1)}, f32[12,8,128]{2,1,0:T(8,128)}) fusion(bf16[128,12,128]{0,2,1:T(8,128)(2,1)} %bitcast.37, bf16[8,1536]{1,0:T(8,128)(2,1)S(1)} %copy-done, pred[]{:T(512)} %get-tuple-element.9), kind=kOutput, calls=%fused_computation.210 | convolution fusion | flops 3182496 | bytes 467329 | tf_op jit(solution)/shard_map/qhd,khd->hqk/dot_general | solution.py:37
  93.8 2.0 %collective-permute-start.9 = (bf16[128,1536]{0,1:T(8,128)(2,1)}, bf16[128,1536]{0,1:T(8,128)(2,1)}, u32[]{:S(2)}, u32[]{:S(2)}) collective-permute-start(bf16[128,1536]{0,1:T(8,128)(2,1)} %copy.101), channel_id=1, source_target_pairs={{0,4},{1,5},{2,6},{3,7},{4,8},{5,9},{6,10},{7,11},{8,12},{9,13},{1... | collective-permute-start | bytes 1179656 | tf_op jit(solution)/shard_map/ppermute | solution.py:20
  95.8 0.9 fusion.88
  96.8 3.2 %collective-permute-start.3 = (bf16[128,1536]{1,0:T(8,128)(2,1)}, bf16[128,1536]{1,0:T(8,128)(2,1)S(1)}, u32[]{:S(2)}, u32[]{:S(2)}) collective-permute-start(bf16[128,1536]{1,0:T(8,128)(2,1)} %param.13), channel_id=1, source_target_pairs={{0,1},{1,2},{2,3},{3,4},{4,5},{5,6},{6,7},{7,8},{8,9},{9,10},{10,1... | collective-permute-start | bytes 1179656 | tf_op jit(solution)/shard_map/ppermute | solution.py:20
  100.0 0.9 fusion.89
  100.9 1.9 %collective-permute-start.5 = (bf16[128,1536]{1,0:T(8,128)(2,1)}, bf16[128,1536]{1,0:T(8,128)(2,1)S(1)}, u32[]{:S(2)}, u32[]{:S(2)}) collective-permute-start(bf16[128,1536]{1,0:T(8,128)(2,1)} %param.13), channel_id=1, source_target_pairs={{1,0},{2,1},{3,2},{4,3},{5,4},{6,5},{7,6},{8,7},{9,8},{10,9},{11,1... | collective-permute-start | bytes 1179656 | tf_op jit(solution)/shard_map/ppermute | solution.py:20
  102.9 0.8 fusion.94
  103.7 0.6 fusion.77
  104.4 0.8 convert_reduce_fusion.6
  105.2 0.8 convert_reduce_fusion.8
  106.0 0.8 convert_reduce_fusion.10
  106.7 0.6 bitcast_maximum_fusion.3
  107.3 0.8 convert_reduce_fusion.14
  108.1 0.7 copy-done.8
  108.8 1.3 collective-permute-start.7
  110.1 1.2 copy.106
  111.4 10.0 %collective-permute-done.3 = bf16[128,1536]{1,0:T(8,128)(2,1)S(1)} collective-permute-done((bf16[128,1536]{1,0:T(8,128)(2,1)}, bf16[128,1536]{1,0:T(8,128)(2,1)S(1)}, u32[]{:S(2)}, u32[]{:S(2)}) %collective-permute-start.3) | collective-permute-done | bytes 393248 | tf_op jit(solution)/shard_map/ppermute | solution.py:20
  121.4 1.3 collective-permute-start.15
  123.0 1.0 convert_reduce_fusion.12
  124.2 0.6 copy-done.19
  124.8 0.7 bitcast_add_fusion
  125.5 1.6 %collective-permute-start.13 = (bf16[128,1536]{0,1:T(8,128)(2,1)}, bf16[128,1536]{0,1:T(8,128)(2,1)}, u32[]{:S(2)}, u32[]{:S(2)}) collective-permute-start(bf16[128,1536]{0,1:T(8,128)(2,1)} %copy.101), channel_id=1, source_target_pairs={{3,0},{4,1},{5,2},{6,3},{7,4},{8,5},{9,6},{10,7},{11,8},{12,9},{13... | collective-permute-start | bytes 1179656 | tf_op jit(solution)/shard_map/ppermute | solution.py:20
  127.3 1.3 fusion.39
  128.7 0.4 convolution_bitcast_fusion.11
  129.4 1.4 convolution_bitcast_fusion.12
  130.9 1.4 fusion.41
  132.3 1.2 copy.121
  135.0 1.4 convolution_bitcast_fusion.6
  136.7 6.1 %collective-permute-done.13 = bf16[128,1536]{0,1:T(8,128)(2,1)} collective-permute-done((bf16[128,1536]{0,1:T(8,128)(2,1)}, bf16[128,1536]{0,1:T(8,128)(2,1)}, u32[]{:S(2)}, u32[]{:S(2)}) %collective-permute-start.13) | collective-permute-done | bytes 393248 | tf_op jit(solution)/shard_map/ppermute | solution.py:20
  142.9 2.1 %multiply_reduce_fusion.1 = (f32[8]{0:T(128)S(1)}, f32[8,12,128]{2,0,1:T(8,128)}) fusion(f32[8,12]{0,1:T(8,128)S(1)} %copy-done.53, f32[8,12,128]{2,0,1:T(8,128)S(1)} %convolution_bitcast_fusion.6, f32[8,12]{0,1:T(8,128)S(1)} %copy-done.54, f32[8,12,128]{2,0,1:T(8,128)S(1)} %fusion.23, bf16[128,12,128]{0,2,1:T(8,128)(2,1)} %bitcast.55, ...), kind=kOutput, calls=%fused_computation.89 | convolution fusion | flops 3244024 | bytes 591008 | tf_op jit(solution)/shard_map/hqk,khd->hqd/dot_general | solution.py:48
  145.0 0.5 add_rsqrt_fusion
  145.5 1.4 fusion.83
  147.2 0.6 copy-done.3
  149.1 0.8 copy-done.1
  150.3 1.3 fusion.6
  152.7 0.7 copy-done.7
  153.4 0.4 multiply_reduce_fusion
  154.1 0.5 copy-done.31
  154.8 0.7 fusion.43
  155.5 0.9 multiply_convert_fusion
  (155 shorter events, 7.7 us)
Async XLA Ops:
  0.6 71.8 %copy-start = (bf16[8,1536]{1,0:T(8,128)(2,1)S(1)}, bf16[8,1536]{1,0:T(8,128)(2,1)}, u32[]{:S(2)}) copy-start(bf16[8,1536]{1,0:T(8,128)(2,1)} %param.14) | copy-start | bytes 73732
  1.9 70.9 %collective-permute-start = (bf16[128,1536]{0,1:T(8,128)(2,1)S(1)}, bf16[128,1536]{0,1:T(8,128)(2,1)S(1)}, u32[]{:S(2)}, u32[]{:S(2)}) collective-permute-start(bf16[128,1536]{0,1:T(8,128)(2,1)S(1)} %copy.98), channel_id=1, source_target_pairs={{0,2},{1,3},{2,4},{3,5},{4,6},{5,7},{6,8},{7,9},{8,10},{9,11},{10,... | collective-permute-start | bytes 1179656 | tf_op jit(solution)/shard_map/ppermute | solution.py:20
  5.9 69.1 %collective-permute-start.6 = (bf16[128,1536]{0,1:T(8,128)(2,1)S(1)}, bf16[128,1536]{0,1:T(8,128)(2,1)}, u32[]{:S(2)}, u32[]{:S(2)}) collective-permute-start(bf16[128,1536]{0,1:T(8,128)(2,1)S(1)} %copy.98), channel_id=1, source_target_pairs={{2,0},{3,1},{4,2},{5,3},{6,4},{7,5},{8,6},{9,7},{10,8},{11,9},{12,... | collective-permute-start | bytes 1179656 | tf_op jit(solution)/shard_map/ppermute | solution.py:20
  7.2 71.0 %collective-permute-start.4 = (bf16[128,1536]{0,1:T(8,128)(2,1)S(1)}, bf16[128,1536]{0,1:T(8,128)(2,1)S(1)}, u32[]{:S(2)}, u32[]{:S(2)}) collective-permute-start(bf16[128,1536]{0,1:T(8,128)(2,1)S(1)} %copy.98), channel_id=1, source_target_pairs={{1,0},{2,1},{3,2},{4,3},{5,4},{6,5},{7,6},{8,7},{9,8},{10,9},{11,1... | collective-permute-start | bytes 1179656 | tf_op jit(solution)/shard_map/ppermute | solution.py:20
  10.0 74.0 %collective-permute-start.2 = (bf16[128,1536]{0,1:T(8,128)(2,1)S(1)}, bf16[128,1536]{0,1:T(8,128)(2,1)S(1)}, u32[]{:S(2)}, u32[]{:S(2)}) collective-permute-start(bf16[128,1536]{0,1:T(8,128)(2,1)S(1)} %copy.98), channel_id=1, source_target_pairs={{0,1},{1,2},{2,3},{3,4},{4,5},{5,6},{6,7},{7,8},{8,9},{9,10},{10,1... | collective-permute-start | bytes 1179656 | tf_op jit(solution)/shard_map/ppermute | solution.py:20
  14.2 72.2 %collective-permute-start.8 = (bf16[128,1536]{0,1:T(8,128)(2,1)S(1)}, bf16[128,1536]{0,1:T(8,128)(2,1)}, u32[]{:S(2)}, u32[]{:S(2)}) collective-permute-start(bf16[128,1536]{0,1:T(8,128)(2,1)S(1)} %copy.98), channel_id=1, source_target_pairs={{0,4},{1,5},{2,6},{3,7},{4,8},{5,9},{6,10},{7,11},{8,12},{9,13},{1... | collective-permute-start | bytes 1179656 | tf_op jit(solution)/shard_map/ppermute | solution.py:20
  19.1 2.6 %copy-start.6 = (bf16[128,1536]{1,0:T(8,128)(2,1)S(1)}, bf16[128,1536]{1,0:T(8,128)(2,1)}, u32[]{:S(2)}) copy-start(bf16[128,1536]{1,0:T(8,128)(2,1)} %param.11) | copy-start | bytes 1179652
  72.7 21.1 %collective-permute-start.14 = (bf16[128,1536]{0,1:T(8,128)(2,1)S(1)}, bf16[128,1536]{0,1:T(8,128)(2,1)S(1)}, u32[]{:S(2)}, u32[]{:S(2)}) collective-permute-start(bf16[128,1536]{0,1:T(8,128)(2,1)S(1)} %copy.98), channel_id=1, source_target_pairs={{4,0},{5,1},{6,2},{7,3},{8,4},{9,5},{10,6},{11,7},{12,8},{13,9},{1... | collective-permute-start | bytes 1179656 | tf_op jit(solution)/shard_map/ppermute | solution.py:20
  75.0 21.8 %collective-permute-start.12 = (bf16[128,1536]{0,1:T(8,128)(2,1)S(1)}, bf16[128,1536]{0,1:T(8,128)(2,1)S(1)}, u32[]{:S(2)}, u32[]{:S(2)}) collective-permute-start(bf16[128,1536]{0,1:T(8,128)(2,1)S(1)} %copy.98), channel_id=1, source_target_pairs={{3,0},{4,1},{5,2},{6,3},{7,4},{8,5},{9,6},{10,7},{11,8},{12,9},{13... | collective-permute-start | bytes 1179656 | tf_op jit(solution)/shard_map/ppermute | solution.py:20
  78.2 25.5 %copy-start.12 = (f32[12,8]{1,0:T(8,128)}, f32[12,8]{1,0:T(8,128)S(1)}, u32[]{:S(2)}) copy-start(f32[12,8]{1,0:T(8,128)S(1)} %get-tuple-element.62) | copy-start | bytes 1156
  78.2 8.2 %copy-start.4 = (bf16[128,1536]{0,1:T(8,128)(2,1)}, bf16[128,1536]{0,1:T(8,128)(2,1)S(1)}, u32[]{:S(2)}) copy-start(bf16[128,1536]{0,1:T(8,128)(2,1)S(1)} %collective-permute-done.4) | copy-start | bytes 1179652
  78.2 22.7 %collective-permute-start.10 = (bf16[128,1536]{0,1:T(8,128)(2,1)S(1)}, bf16[128,1536]{0,1:T(8,128)(2,1)S(1)}, u32[]{:S(2)}, u32[]{:S(2)}) collective-permute-start(bf16[128,1536]{0,1:T(8,128)(2,1)S(1)} %copy.98), channel_id=1, source_target_pairs={{0,3},{1,4},{2,5},{3,6},{4,7},{5,8},{6,9},{7,10},{8,11},{9,12},{10... | collective-permute-start | bytes 1179656 | tf_op jit(solution)/shard_map/ppermute | solution.py:20
  84.1 19.6 %copy-start.18 = (f32[12,8]{1,0:T(8,128)}, f32[12,8]{1,0:T(8,128)S(1)}, u32[]{:S(2)}) copy-start(f32[12,8]{1,0:T(8,128)S(1)} %get-tuple-element.64) | copy-start | bytes 1156
  84.1 9.7 %copy-start.2 = (bf16[128,1536]{0,1:T(8,128)(2,1)}, bf16[128,1536]{0,1:T(8,128)(2,1)S(1)}, u32[]{:S(2)}) copy-start(bf16[128,1536]{0,1:T(8,128)(2,1)S(1)} %collective-permute-done.2) | copy-start | bytes 1179652
  84.1 24.0 %collective-permute-start.1 = (bf16[128,1536]{1,0:T(8,128)(2,1)}, bf16[128,1536]{1,0:T(8,128)(2,1)S(1)}, u32[]{:S(2)}, u32[]{:S(2)}) collective-permute-start(bf16[128,1536]{1,0:T(8,128)(2,1)} %param.13), channel_id=1, source_target_pairs={{0,2},{1,3},{2,4},{3,5},{4,6},{5,7},{6,8},{7,9},{8,10},{9,11},{10,... | collective-permute-start | bytes 1179656 | tf_op jit(solution)/shard_map/ppermute | solution.py:20
  86.4 42.7 %collective-permute-start.11 = (bf16[128,1536]{0,1:T(8,128)(2,1)}, bf16[128,1536]{0,1:T(8,128)(2,1)}, u32[]{:S(2)}, u32[]{:S(2)}) collective-permute-start(bf16[128,1536]{0,1:T(8,128)(2,1)} %copy.101), channel_id=1, source_target_pairs={{0,3},{1,4},{2,5},{3,6},{4,7},{5,8},{6,9},{7,10},{8,11},{9,12},{10... | collective-permute-start | bytes 1179656 | tf_op jit(solution)/shard_map/ppermute | solution.py:20
  93.8 37.0 %collective-permute-start.9 = (bf16[128,1536]{0,1:T(8,128)(2,1)}, bf16[128,1536]{0,1:T(8,128)(2,1)}, u32[]{:S(2)}, u32[]{:S(2)}) collective-permute-start(bf16[128,1536]{0,1:T(8,128)(2,1)} %copy.101), channel_id=1, source_target_pairs={{0,4},{1,5},{2,6},{3,7},{4,8},{5,9},{6,10},{7,11},{8,12},{9,13},{1... | collective-permute-start | bytes 1179656 | tf_op jit(solution)/shard_map/ppermute | solution.py:20
  96.8 6.9 %copy-start.25 = (f32[12,8]{1,0:T(8,128)}, f32[12,8]{1,0:T(8,128)S(1)}, u32[]{:S(2)}) copy-start(f32[12,8]{1,0:T(8,128)S(1)} %get-tuple-element.58) | copy-start | bytes 1156
  96.8 24.6 %collective-permute-start.3 = (bf16[128,1536]{1,0:T(8,128)(2,1)}, bf16[128,1536]{1,0:T(8,128)(2,1)S(1)}, u32[]{:S(2)}, u32[]{:S(2)}) collective-permute-start(bf16[128,1536]{1,0:T(8,128)(2,1)} %param.13), channel_id=1, source_target_pairs={{0,1},{1,2},{2,3},{3,4},{4,5},{5,6},{6,7},{7,8},{8,9},{9,10},{10,1... | collective-permute-start | bytes 1179656 | tf_op jit(solution)/shard_map/ppermute | solution.py:20
  100.9 2.8 %copy-start.29 = (f32[12,8]{1,0:T(8,128)}, f32[12,8]{1,0:T(8,128)S(1)}, u32[]{:S(2)}) copy-start(f32[12,8]{1,0:T(8,128)S(1)} %get-tuple-element.60) | copy-start | bytes 1156
  100.9 3.5 %copy-start.9 = (f32[12,8,128]{2,1,0:T(8,128)}, f32[12,8,128]{2,1,0:T(8,128)S(1)}, u32[]{:S(2)}) copy-start(f32[12,8,128]{2,1,0:T(8,128)S(1)} %get-tuple-element.61) | copy-start | bytes 147460
  100.9 24.5 %collective-permute-start.5 = (bf16[128,1536]{1,0:T(8,128)(2,1)}, bf16[128,1536]{1,0:T(8,128)(2,1)S(1)}, u32[]{:S(2)}, u32[]{:S(2)}) collective-permute-start(bf16[128,1536]{1,0:T(8,128)(2,1)} %param.13), channel_id=1, source_target_pairs={{1,0},{2,1},{3,2},{4,3},{5,4},{6,5},{7,6},{8,7},{9,8},{10,9},{11,1... | collective-permute-start | bytes 1179656 | tf_op jit(solution)/shard_map/ppermute | solution.py:20
  104.3 0.8 copy-start.16
  104.3 0.8 copy-start.35
  104.3 0.8 copy-start.14
  104.3 0.8 copy-start.20
  104.3 1.6 %copy-start.22 = (f32[12,8]{1,0:T(8,128)}, f32[12,8]{1,0:T(8,128)S(1)}, u32[]{:S(2)}) copy-start(f32[12,8]{1,0:T(8,128)S(1)} %get-tuple-element.24) | copy-start | bytes 1156
  104.4 1.6 %copy-start.27 = (f32[12,8]{1,0:T(8,128)}, f32[12,8]{1,0:T(8,128)S(1)}, u32[]{:S(2)}) copy-start(f32[12,8]{1,0:T(8,128)S(1)} %get-tuple-element.25) | copy-start | bytes 1156
  104.4 3.0 %copy-start.46 = (f32[12,8]{1,0:T(8,128)}, f32[12,8]{1,0:T(8,128)S(1)}, u32[]{:S(2)}) copy-start(f32[12,8]{1,0:T(8,128)S(1)} %get-tuple-element.41) | copy-start | bytes 1156
  108.8 23.4 %collective-permute-start.7 = (bf16[128,1536]{1,0:T(8,128)(2,1)}, bf16[128,1536]{1,0:T(8,128)(2,1)}, u32[]{:S(2)}, u32[]{:S(2)}) collective-permute-start(bf16[128,1536]{1,0:T(8,128)(2,1)} %param.13), channel_id=1, source_target_pairs={{2,0},{3,1},{4,2},{5,3},{6,4},{7,5},{8,6},{9,7},{10,8},{11,9},{12,... | collective-permute-start | bytes 1179656 | tf_op jit(solution)/shard_map/ppermute | solution.py:20
  121.4 13.2 %collective-permute-start.15 = (bf16[128,1536]{0,1:T(8,128)(2,1)}, bf16[128,1536]{0,1:T(8,128)(2,1)}, u32[]{:S(2)}, u32[]{:S(2)}) collective-permute-start(bf16[128,1536]{0,1:T(8,128)(2,1)} %copy.101), channel_id=1, source_target_pairs={{4,0},{5,1},{6,2},{7,3},{8,4},{9,5},{10,6},{11,7},{12,8},{13,9},{1... | collective-permute-start | bytes 1179656 | tf_op jit(solution)/shard_map/ppermute | solution.py:20
  122.9 1.2 copy-start.26
  122.9 1.2 copy-start.30
  122.9 1.2 copy-start.38
  122.9 1.2 copy-start.39
  122.9 1.2 copy-start.40
  122.9 1.2 copy-start.41
  123.0 1.2 copy-start.42
  123.0 1.2 copy-start.43
  123.0 1.2 copy-start.44
  123.0 1.2 copy-start.45
  123.0 1.2 copy-start.48
  125.4 1.9 %copy-start.47 = (f32[12,8]{1,0:T(8,128)S(1)}, f32[12,8]{1,0:T(8,128)}, u32[]{:S(2)}) copy-start(f32[12,8]{1,0:T(8,128)} %copy-done.46) | copy-start | bytes 1156
  125.5 1.9 %copy-start.58 = (f32[8,12]{0,1:T(8,128)S(1)}, f32[8,12]{0,1:T(8,128)}, u32[]{:S(2)}) copy-start(f32[8,12]{0,1:T(8,128)} %get-tuple-element.38) | copy-start | bytes 1156
  125.5 1.9 %copy-start.59 = (f32[8,12]{0,1:T(8,128)S(1)}, f32[8,12]{0,1:T(8,128)}, u32[]{:S(2)}) copy-start(f32[8,12]{0,1:T(8,128)} %get-tuple-element.40) | copy-start | bytes 1156
  125.5 17.4 %collective-permute-start.13 = (bf16[128,1536]{0,1:T(8,128)(2,1)}, bf16[128,1536]{0,1:T(8,128)(2,1)}, u32[]{:S(2)}, u32[]{:S(2)}) collective-permute-start(bf16[128,1536]{0,1:T(8,128)(2,1)} %copy.101), channel_id=1, source_target_pairs={{3,0},{4,1},{5,2},{6,3},{7,4},{8,5},{9,6},{10,7},{11,8},{12,9},{13... | collective-permute-start | bytes 1179656 | tf_op jit(solution)/shard_map/ppermute | solution.py:20
  127.3 1.4 copy-start.28
  129.4 1.4 copy-start.11
  129.4 1.4 copy-start.37
  129.4 1.5 copy-start.55
  129.4 1.5 copy-start.56
  129.4 1.5 copy-start.57
  132.3 1.3 copy-start.23
  132.3 1.3 copy-start.34
  135.0 1.4 copy-start.15
  135.0 1.4 copy-start.32
  136.3 6.5 %copy-start.10 = (f32[12,8,128]{2,1,0:T(8,128)S(1)}, f32[12,8,128]{2,1,0:T(8,128)}, u32[]{:S(2)}) copy-start(f32[12,8,128]{2,1,0:T(8,128)} %copy-done.9) | copy-start | bytes 147460
  136.3 6.5 %copy-start.36 = (f32[12,8]{1,0:T(8,128)S(1)}, f32[12,8]{1,0:T(8,128)}, u32[]{:S(2)}) copy-start(f32[12,8]{1,0:T(8,128)} %copy-done.35) | copy-start | bytes 1156
  136.4 6.5 %copy-start.53 = (f32[8,12]{0,1:T(8,128)S(1)}, f32[8,12]{0,1:T(8,128)}, u32[]{:S(2)}) copy-start(f32[8,12]{0,1:T(8,128)} %get-tuple-element.10) | copy-start | bytes 1156
  136.4 6.5 %copy-start.54 = (f32[8,12]{0,1:T(8,128)S(1)}, f32[8,12]{0,1:T(8,128)}, u32[]{:S(2)}) copy-start(f32[8,12]{0,1:T(8,128)} %get-tuple-element.11) | copy-start | bytes 1156
  145.5 1.4 copy-start.5
  146.9 1.0 copy-start.3
  148.8 1.1 copy-start.1
  152.4 1.0 copy-start.7
  (15 other events, 10.7 us)
where the time goes:
time: 158 us; the launch traced here: 156 us
  blocking collectives  45.6 us (29%)
  starting transfers between devices  41.7 us (26%)
  matrix products  25.7 us (16%)
  waiting for transfers between devices  16.2 us (10%)
  local copies, waits for them, and re-layouts  15.2 us (10%)
  other arithmetic  9.86 us (6%)
  between operations  2.14 us (1%)
    ppermute x16, starting transfers between devices, passed_along(): lax.ppermute(value, axis, [(source, source + steps) for source in range(f...  41.7 us
    all_gather x1, blocking collectives, on_device(): lax.all_gather(audio_k, 'seq', axis=0, tiled=True)  23.8 us
    all_gather x1, blocking collectives, on_device(): lax.all_gather(audio_v, 'seq', axis=0, tiled=True)  21.8 us
    ppermute x16, waiting for transfers between devices, passed_along(): lax.ppermute(value, axis, [(source, source + steps) for source in range(f...  16.2 us
    dot_general x15, matrix products, attend_block(): jnp.einsum('qhd,khd->hqk', split_heads(queries), split_heads(key_block),...  14 us
    dot_general x15, matrix products, attend_block(): jnp.einsum('hqk,khd->hqd', weights, split_heads(value_block), preferred_e...  11.7 us
    unnamed x129, local copies, waits for them, and re-layouts  10.9 us
    reduce_sum x8, other arithmetic, attend_block(): jnp.sum(weights.astype(jnp.float32), axis=-1)  4.97 us
  transfers between devices with their start and end apart: 16, of which 2 were waited for; matrix products, arithmetic and copies ran while one was open for 20% of the time, Pallas kernels for 0%

commit v1 on v0

v1 whole, which is shorter than its diff:
```python
import functools

import jax
import jax.numpy as jnp
from jax import lax
from jax.experimental import pallas as pl
from jax.experimental.pallas import tpu as pltpu
from jax.sharding import PartitionSpec as P

HD = 128
RMAX = 2
SPAN = 4
LOG2E = 1.4426950408889634
SCALE = HD ** (-0.5) * LOG2E
NEG = -1e30
EPS = 1e-6
MESH = pl.DeviceIdType.MESH
LAG_Z = 1
LAG_C = 2


def kernel(
    n, heads, tok, aud, lmax,
    radius, tile_list, tile_count,
    vq_hbm, vk_hbm, vv_hbm, aq_hbm, ak_hbm, av_hbm, vgain, again,
    vout, aout,
    kv, audio, qown, aqown, aqin, qx, qr, part_o, part_s, back_o, back_s, attn, aattn,
    load_sem, s_dk, r_dk, s_y, r_y, s_z, r_z, s_dy, r_dy, s_dz, r_dz,
    s_aud, r_aud, s_daud, r_daud, s_q, r_q, s_bo, r_bo, s_bs, r_bs,
):
    me = lax.axis_index("seq")
    chips = n // 2
    chip = me // 2
    core = me % 2
    mate = chip * 2 + (1 - core)
    odd = chip % 2
    across_chip = chip + 1 - 2 * odd
    across = across_chip * 2 + core
    step = 2 - 4 * odd
    fwd_chip = chip + step
    has_fwd = (fwd_chip >= 0) & (fwd_chip < chips)
    src_chip = chip - step
    has_src = (src_chip >= 0) & (src_chip < chips)
    zchip = chip - 1 + 2 * odd
    fwd = jnp.clip(fwd_chip, 0, chips - 1) * 2 + core

    barrier = pltpu.get_barrier_semaphore()

    def greet(i, _):
        pl.semaphore_signal(barrier, inc=1, device_id={"seq": (me + i) % n}, device_id_type=MESH)
        return 0

    lax.fori_loop(1, n, greet, 0)

    loads = [
        pltpu.make_async_copy(aq_hbm, aqown, load_sem.at[0]),
        pltpu.make_async_copy(ak_hbm, audio.at[me, 0], load_sem.at[1]),
        pltpu.make_async_copy(av_hbm, audio.at[me, 1], load_sem.at[2]),
        pltpu.make_async_copy(vk_hbm, kv.at[0, pl.ds(0, tok)], load_sem.at[3]),
        pltpu.make_async_copy(vv_hbm, kv.at[1, pl.ds(0, tok)], load_sem.at[4]),
        pltpu.make_async_copy(vq_hbm, qown, load_sem.at[5]),
    ]
    for load in loads:
        load.start()
    @pl.when(jnp.logical_not(has_src))
    def _():
        kv[:, pl.ds(4 * tok, 2 * tok), :] = jnp.zeros((2, 2 * tok, heads * HD), kv.dtype)

    far = []
    for slot in range(4):
        far_chip = chip + (2 if slot < 2 else -2)
        exists = (far_chip >= 0) & (far_chip < chips)
        device = jnp.clip(far_chip, 0, chips - 1) * 2 + slot % 2
        there = (2 if slot < 2 else 0) + core
        far.append((slot, exists, device, there))

        @pl.when(jnp.logical_not(exists))
        def _(slot=slot):
            aqin[slot] = jnp.zeros(aqin.shape[1:], aqin.dtype)
            back_o[slot] = jnp.zeros(back_o.shape[1:], back_o.dtype)
            back_s[slot] = jnp.zeros(back_s.shape[1:], back_s.dtype)

    pl.semaphore_wait(barrier, n - 1)

    def remote(src, dst, s, r, device):
        return pltpu.make_async_remote_copy(
            src_ref=src, dst_ref=dst, send_sem=s, recv_sem=r,
            device_id={"seq": device}, device_id_type=MESH)

    def q_copy(slot, device, there):
        return remote(aqown, aqin.at[there], s_q.at[slot], r_q.at[there], device)

    def q_arrival(slot):
        return remote(aqown, aqin.at[slot], s_q.at[slot], r_q.at[slot], mate)

    loads[0].wait()
    for slot, exists, device, there in far:
        @pl.when(exists)
        def _(slot=slot, device=device, there=there):
            q_copy(slot, device, there).start()
    loads[1].wait()
    loads[2].wait()

    def aud_copy(block, device, i):
        return remote(audio.at[block], audio.at[block], s_aud.at[i], r_aud.at[block], device)

    def daud_copy(block, i):
        return remote(audio.at[block], audio.at[block], s_daud.at[i], r_daud.at[block], mate)

    def send_audio(i, _):
        aud_copy(me, (me + 2 * i) % n, i).start()
        return 0

    lax.fori_loop(1, chips, send_audio, 0)
    daud_copy(me, 0).start()
    loads[3].wait()
    loads[4].wait()

    def cols(h):
        return pl.ds(pl.multiple_of(h * HD, HD), HD)

    def kv_head(slot, h):
        return kv.at[:, pl.ds(slot * tok, tok), cols(h)]

    def y_copy(h):
        return remote(kv_head(0, h), kv_head(2, h), s_y.at[h], r_y.at[h], across)

    def z_copy(h):
        return remote(kv_head(2, h), kv_head(4, h), s_z.at[h], r_z.at[h], fwd)

    def dy_copy(h):
        return remote(kv_head(2, h), kv_head(3, h), s_dy.at[h], r_dy.at[h], mate)

    def dz_copy(h):
        return remote(kv_head(4, h), kv_head(5, h), s_dz.at[h], r_dz.at[h], mate)

    dk = remote(kv.at[:, pl.ds(0, tok)], kv.at[:, pl.ds(tok, tok)], s_dk, r_dk, mate)

    def send_y(h, _):
        y_copy(h).start()
        return 0

    lax.fori_loop(0, heads, send_y, 0)
    dk.start()

    loads[5].wait()
    wide = jnp.concatenate([aqown[...].astype(jnp.float32), jnp.zeros((aud, heads * HD), jnp.float32)], axis=0)
    qx[...] = wide.astype(jnp.bfloat16)

    for slot, exists, device, there in far:
        @pl.when(exists)
        def _(slot=slot):
            q_arrival(slot).wait_recv()
    for pair in range(2):
        both = jnp.concatenate(
            [aqin[2 * pair].astype(jnp.float32), aqin[2 * pair + 1].astype(jnp.float32)], axis=0)
        qr[pl.ds(2 * aud * pair, 2 * aud), :] = both.astype(jnp.bfloat16)
    lane = lax.broadcasted_iota(jnp.int32, (4 * aud, HD), 1)
    part_s[...] = jnp.zeros(part_s.shape, jnp.float32)

    def dot_t(a, b):
        return lax.dot_general(a, b, (((1,), (1,)), ((), ())), preferred_element_type=jnp.float32)

    def far_head(h, _):
        s = dot_t(qr[:, cols(h)], kv[0, pl.ds(0, tok), cols(h)]) * SCALE
        m = jnp.max(s, axis=1, keepdims=True)
        w = jnp.exp2(s - m).astype(jnp.bfloat16)
        total = jnp.sum(w.astype(jnp.float32), axis=1, keepdims=True)
        o = jnp.dot(w, kv[1, pl.ds(0, tok), cols(h)], preferred_element_type=jnp.float32) / total
        for slot in range(4):
            rows = slice(slot * aud, (slot + 1) * aud)
            part_o[slot, :, cols(h)] = o[rows].astype(part_o.dtype)
            st = part_s[slot]
            st = jnp.where(lane[rows] == h, m[rows], st)
            st = jnp.where(lane[rows] == h + 64, total[rows], st)
            part_s[slot] = st
        return 0

    lax.fori_loop(0, heads, far_head, 0)

    def bo_copy(slot, device, there):
        return remote(part_o.at[slot], back_o.at[there], s_bo.at[slot], r_bo.at[there], device)

    def bs_copy(slot, device, there):
        return remote(part_s.at[slot], back_s.at[there], s_bs.at[slot], r_bs.at[there], device)

    for slot, exists, device, there in far:
        @pl.when(exists)
        def _(slot=slot, device=device, there=there):
            bo_copy(slot, device, there).start()
            bs_copy(slot, device, there).start()

    def pass_audio(i, _):
        block = (me + 2 * i) % n
        aud_copy(block, mate, i).wait_recv()
        daud_copy(block, i).start()
        return 0

    lax.fori_loop(1, chips, pass_audio, 0)

    def take_audio(i, _):
        daud_copy((mate + 2 * i) % n, i).wait_recv()
        return 0

    lax.fori_loop(0, chips, take_audio, 0)

    def lay_audio(i, _):
        for j in range(2):
            pair = jnp.concatenate(
                [audio[2 * i, j].astype(jnp.float32), audio[2 * i + 1, j].astype(jnp.float32)], axis=0)
            kv[j, pl.ds(pl.multiple_of(6 * tok + 2 * aud * i, 2 * aud), 2 * aud), :] = pair.astype(jnp.bfloat16)
        return 0

    lax.fori_loop(0, chips, lay_audio, 0)

    for slot, exists, device, there in far:
        @pl.when(exists)
        def _(slot=slot):
            bo_copy(slot, mate, slot).wait_recv()
            bs_copy(slot, mate, slot).wait_recv()
    dk.wait_recv()

    near = radius[0]
    count = tile_count[me]

    def is_listed(tile):
        listed = jnp.int32(0)
        for j in range(lmax):
            listed = jnp.where((tile_list[me, j] == tile) & (j < count), 1, listed)
        return listed > 0

    tiles = [me, mate, across, across_chip * 2 + 1 - core, zchip * 2 + core, zchip * 2 + 1 - core]
    see_v, see_a = [], []
    for tile in tiles:
        inside = (tile >= 0) & (tile < n)
        see_v.append(jnp.where(inside & (jnp.abs(tile - me) <= near), 0.0, NEG).astype(jnp.float32))
        see_a.append(jnp.where(inside & is_listed(tile), 0.0, NEG).astype(jnp.float32))
    far_seen = []
    for slot in range(4):
        tile = (chip + (2 if slot < 2 else -2)) * 2 + slot % 2
        ok = (tile >= 0) & (tile < n) & is_listed(tile)
        far_seen.append(jnp.where(ok, 0.0, NEG).astype(jnp.float32))

    span = 6 * tok
    keys = span + n * aud
    lane8 = lax.broadcasted_iota(jnp.int32, (aud, HD), 1)

    def softmax_part(s, biases):
        blocks = [s[:, i * tok:(i + 1) * tok] * SCALE + biases[i] for i in range(len(biases))]
        if s.shape[1] > len(biases) * tok:
            blocks.append(s[:, len(biases) * tok:] * SCALE)
        m = functools.reduce(jnp.maximum, [jnp.max(b, axis=1, keepdims=True) for b in blocks]) if blocks[-1].shape[1] != tok else jnp.max(functools.reduce(jnp.maximum, blocks), axis=1, keepdims=True)
        w = jnp.concatenate([jnp.exp2(b - m).astype(jnp.bfloat16) for b in blocks], axis=1)
        return m, w

    def head(h):
        q = jnp.concatenate([qown[:, cols(h)], qx[:, cols(h)]], axis=0)
        s = dot_t(q, kv[0, :, cols(h)])
        _, wv = softmax_part(s[:tok], see_v)
        ma, wa = softmax_part(s[tok:, :span], see_a)
        wa = jnp.concatenate([wa, jnp.zeros((2 * aud, keys - span), jnp.bfloat16)], axis=1)
        w = jnp.concatenate([wv, wa], axis=0)
        v = kv[1, :, cols(h)]
        o = jnp.dot(w, jnp.concatenate([v, jnp.ones((keys, HD), jnp.bfloat16)], axis=1), preferred_element_type=jnp.float32)
        attn[:, cols(h)] = o[:tok, :HD] / o[:tok, HD:]
        oa = o[tok:tok + aud, :HD]
        la = o[tok:tok + aud, HD:]
        ma = ma[:aud]
        peaks, sums = [], []
        for slot in range(4):
            st = back_s[slot]
            peaks.append(jnp.max(jnp.where(lane8 == h, st, NEG), axis=1, keepdims=True) + far_seen[slot])
            sums.append(jnp.sum(jnp.where(lane8 == h + 64, st, 0.0), axis=1, keepdims=True))
        peak = functools.reduce(jnp.maximum, peaks, ma)
        shrink = jnp.exp2(ma - peak)
        oa = oa * shrink
        la = la * shrink
        for slot in range(4):
            share = jnp.exp2(peaks[slot] - peak) * sums[slot]
            oa = oa + back_o[slot, :, cols(h)].astype(jnp.float32) * share
            la = la + share
        aattn[:, cols(h)] = oa / la

    def relay(i, _):
        @pl.when(i < heads)
        def _():
            y_copy(i).wait_recv()

            @pl.when(has_fwd)
            def _():
                z_copy(i).start()
            dy_copy(i).start()

        @pl.when((i >= LAG_Z) & (i < heads + LAG_Z) & has_src)
        def _():
            z_copy(i - LAG_Z).wait_recv()
            dz_copy(i - LAG_Z).start()

        @pl.when(i >= LAG_C)
        def _():
            h = i - LAG_C
            dy_copy(h).wait_recv()

            @pl.when(has_src)
            def _():
                dz_copy(h).wait_recv()
            head(h)
        return 0

    lax.fori_loop(0, heads + LAG_C, relay, 0)

    def finish(mixed, gain):
        scale = lax.rsqrt(jnp.mean(mixed * mixed, axis=1, keepdims=True) + EPS)
        return (mixed * scale * gain).astype(jnp.bfloat16)

    vout[...] = finish(attn[...], vgain[...].reshape(1, heads * HD))
    aout[...] = finish(aattn[...], again[...].reshape(1, heads * HD))

    for slot, exists, device, there in far:
        @pl.when(exists)
        def _(slot=slot, device=device, there=there):
            q_copy(slot, device, there).wait_send()
            bo_copy(slot, device, there).wait_send()
            bs_copy(slot, device, there).wait_send()

    def audio_left(i, _):
        aud_copy(me, mate, i).wait_send()
        return 0

    lax.fori_loop(1, chips, audio_left, 0)

    def daudio_left(i, _):
        daud_copy(me, i).wait_send()
        return 0

    lax.fori_loop(0, chips, daudio_left, 0)
    dk.wait_send()

    def heads_left(h, _):
        y_copy(h).wait_send()
        dy_copy(h).wait_send()

        @pl.when(has_fwd)
        def _():
            z_copy(h).wait_send()

        @pl.when(has_src)
        def _():
            dz_copy(h).wait_send()
        return 0

    lax.fori_loop(0, heads, heads_left, 0)


def solution(mesh):
    n = mesh.shape["seq"]
    chips = n // 2

    def on_device(vq, vk, vv, aq, ak, av, radius, tile_list, tile_count, vgain, again):
        tok, width = vq.shape
        aud = aq.shape[0]
        heads = width // HD
        keys = 6 * tok + n * aud
        bf, f32 = jnp.bfloat16, jnp.float32
        dma = pltpu.SemaphoreType.DMA
        per_head = dma((heads,))
        smem = pl.BlockSpec(memory_space=pltpu.SMEM)
        anyw = pl.BlockSpec(memory_space=pl.ANY)
        vmem = pl.BlockSpec(memory_space=pltpu.VMEM)
        return pl.pallas_call(
            functools.partial(kernel, n, heads, tok, aud, tile_list.shape[1]),
            out_shape=(jax.ShapeDtypeStruct(vq.shape, bf), jax.ShapeDtypeStruct(aq.shape, bf)),
            in_specs=[smem] * 3 + [anyw] * 6 + [vmem] * 2,
            out_specs=(vmem, vmem),
            scratch_shapes=[
                pltpu.VMEM((2, keys, width), bf),
                pltpu.VMEM((n, 2, aud, width), bf),
                pltpu.VMEM((tok, width), bf),
                pltpu.VMEM((aud, width), bf),
                pltpu.VMEM((4, aud, width), bf),
                pltpu.VMEM((2 * aud, width), bf),
                pltpu.VMEM((4 * aud, width), bf),
                pltpu.VMEM((4, aud, width), bf),
                pltpu.VMEM((4, aud, HD), f32),
                pltpu.VMEM((4, aud, width), bf),
                pltpu.VMEM((4, aud, HD), f32),
                pltpu.VMEM((tok, width), f32),
                pltpu.VMEM((aud, width), f32),
                dma((6,)), dma, dma,
                *([per_head] * 8),
                dma((chips,)), dma((n,)), dma((chips,)), dma((n,)),
                *([dma((4,))] * 6),
            ],
            compiler_params=pltpu.CompilerParams(
                collective_id=0, has_side_effects=True, vmem_limit_bytes=48 * 1024 * 1024),
        )(radius, tile_list, tile_count, vq, vk, vv, aq, ak, av, vgain, again)

    rows = P(("clips", "seq"), None)
    return jax.shard_map(
        on_device,
        mesh=mesh,
        in_specs=(rows,) * 6 + (P(("clips", "seq")), P("clips", None), P("clips"), P(), P()),
        out_specs=(rows, rows),
        check_vma=False,
    )
```

time: 158 us -> 53.7 us (0.34)
  the two profiles are of different devices: /device:TPU:1 before, /device:TPU:5 now
where the time goes in v1:
time: 53.7 us; the launch traced here: 53.2 us
  Pallas kernels  43.8 us (82%)
  local copies, waits for them, and re-layouts  8.03 us (15%)
  between operations  1.32 us (2%)
    pallas_call x1, Pallas kernels, on_device(): pl.pallas_call(functools.partial(kernel, n, heads, tok, aud, tile_list.sh...  43.8 us
    unnamed x21, local copies, waits for them, and re-layouts  8.03 us

profile of v1, /device:TPU:5, one launch (start us, length us, event | category | flops | bytes accessed | tf_op | source)
XLA Modules:
  0.0 53.2 jit_solution(15450633771442864475)
XLA Ops:
  0.6 0.0 copy-start.6
  1.3 0.0 copy-start.8
  1.3 0.8 %copy.13.tile_list = s32[16,5]{1,0:T(8,128)S(1)} copy(s32[16,5]{0,1:T(8,128)} %param.18) | data formatting | bytes 640 | tf_op args[7]
  2.1 0.0 copy-done.6
  2.1 0.0 copy-done.8
  2.1 0.0 copy-start
  2.1 1.0 %copy-done = bf16[128,1536]{1,0:T(8,128)(2,1)S(1)} copy-done((bf16[128,1536]{1,0:T(8,128)(2,1)S(1)}, bf16[128,1536]{1,0:T(8,128)(2,1)}, u32[]{:S(2)}) %copy-start) | copy-done | bytes 393240
  3.1 0.0 copy-start.1
  3.1 1.0 %copy-done.1 = bf16[128,1536]{1,0:T(8,128)(2,1)S(1)} copy-done((bf16[128,1536]{1,0:T(8,128)(2,1)S(1)}, bf16[128,1536]{1,0:T(8,128)(2,1)}, u32[]{:S(2)}) %copy-start.1) | copy-done | bytes 393240
  4.1 0.0 copy-start.2
  4.1 1.0 %copy-done.2 = bf16[128,1536]{1,0:T(8,128)(2,1)S(1)} copy-done((bf16[128,1536]{1,0:T(8,128)(2,1)S(1)}, bf16[128,1536]{1,0:T(8,128)(2,1)}, u32[]{:S(2)}) %copy-start.2) | copy-done | bytes 393240
  5.1 0.0 copy-start.3
  5.1 0.7 %copy-done.3 = bf16[8,1536]{1,0:T(8,128)(2,1)S(1)} copy-done((bf16[8,1536]{1,0:T(8,128)(2,1)S(1)}, bf16[8,1536]{1,0:T(8,128)(2,1)}, u32[]{:S(2)}) %copy-start.3) | copy-done | bytes 24600
  5.8 0.0 copy-start.4
  5.8 0.7 %copy-done.4 = bf16[8,1536]{1,0:T(8,128)(2,1)S(1)} copy-done((bf16[8,1536]{1,0:T(8,128)(2,1)S(1)}, bf16[8,1536]{1,0:T(8,128)(2,1)}, u32[]{:S(2)}) %copy-start.4) | copy-done | bytes 24600
  6.6 0.0 copy-start.5
  6.6 0.7 %copy-done.5 = bf16[8,1536]{1,0:T(8,128)(2,1)S(1)} copy-done((bf16[8,1536]{1,0:T(8,128)(2,1)S(1)}, bf16[8,1536]{1,0:T(8,128)(2,1)}, u32[]{:S(2)}) %copy-start.5) | copy-done | bytes 24600
  7.3 0.0 copy-start.7
  7.3 0.7 %copy-done.7 = f32[1536]{0:T(1024)S(1)} copy-done((f32[1536]{0:T(1024)S(1)}, f32[1536]{0:T(1024)}, u32[]{:S(2)}) %copy-start.7) | copy-done | bytes 6168
  8.0 43.8 %shard_map.122 = (bf16[128,1536]{1,0:T(8,128)(2,1)S(1)}, bf16[8,1536]{1,0:T(8,128)(2,1)S(1)}) custom-call(s32[1]{0:T(128)S(6)} %copy.16.radius, s32[16,5]{1,0:T(8,128)S(1)} %copy.13.tile_list, s32[16]{0:T(128)S(1)} %copy-done.8, bf16[128,1536]{1,0:T(8,128)(2,1)S(1)} %copy-done, bf16[128,1536]{1,0:T(8,128)(2,1)S(1)} %copy-done.1, ...), custom_call_target="tpu_custom_call" | custom-call | tf_op jit(solution)/shard_map/pallas_call | solution.py:370
  51.8 0.7 %copy.17 = bf16[128,1536]{1,0:T(8,128)(2,1)} copy(bf16[128,1536]{1,0:T(8,128)(2,1)S(1)} %get-tuple-element.4) | data formatting | bytes 786432
  52.6 0.6 %copy.18 = bf16[8,1536]{1,0:T(8,128)(2,1)} copy(bf16[8,1536]{1,0:T(8,128)(2,1)S(1)} %get-tuple-element.5) | data formatting | bytes 49152
Async XLA Ops:
  0.6 1.5 %copy-start.6 = (f32[1536]{0:T(1024)S(1)}, f32[1536]{0:T(1024)}, u32[]{:S(2)}) copy-start(f32[1536]{0:T(1024)} %vgain.1) | copy-start | bytes 18436
  1.3 0.8 %copy-start.8 = (s32[16]{0:T(128)S(1)}, s32[16]{0:T(128)}, u32[]{:S(2)}) copy-start(s32[16]{0:T(128)} %tile_count.1) | copy-start | bytes 196
  2.1 1.0 %copy-start = (bf16[128,1536]{1,0:T(8,128)(2,1)S(1)}, bf16[128,1536]{1,0:T(8,128)(2,1)}, u32[]{:S(2)}) copy-start(bf16[128,1536]{1,0:T(8,128)(2,1)} %vq_hbm.1) | copy-start | bytes 1179652
  3.1 1.0 %copy-start.1 = (bf16[128,1536]{1,0:T(8,128)(2,1)S(1)}, bf16[128,1536]{1,0:T(8,128)(2,1)}, u32[]{:S(2)}) copy-start(bf16[128,1536]{1,0:T(8,128)(2,1)} %vk_hbm.1) | copy-start | bytes 1179652
  4.1 1.0 %copy-start.2 = (bf16[128,1536]{1,0:T(8,128)(2,1)S(1)}, bf16[128,1536]{1,0:T(8,128)(2,1)}, u32[]{:S(2)}) copy-start(bf16[128,1536]{1,0:T(8,128)(2,1)} %vv_hbm.1) | copy-start | bytes 1179652
  5.1 0.7 %copy-start.3 = (bf16[8,1536]{1,0:T(8,128)(2,1)S(1)}, bf16[8,1536]{1,0:T(8,128)(2,1)}, u32[]{:S(2)}) copy-start(bf16[8,1536]{1,0:T(8,128)(2,1)} %aq_hbm.1) | copy-start | bytes 73732
  5.8 0.7 %copy-start.4 = (bf16[8,1536]{1,0:T(8,128)(2,1)S(1)}, bf16[8,1536]{1,0:T(8,128)(2,1)}, u32[]{:S(2)}) copy-start(bf16[8,1536]{1,0:T(8,128)(2,1)} %ak_hbm.1) | copy-start | bytes 73732
  6.6 0.7 %copy-start.5 = (bf16[8,1536]{1,0:T(8,128)(2,1)S(1)}, bf16[8,1536]{1,0:T(8,128)(2,1)}, u32[]{:S(2)}) copy-start(bf16[8,1536]{1,0:T(8,128)(2,1)} %av_hbm.1) | copy-start | bytes 73732
  7.3 0.7 %copy-start.7 = (f32[1536]{0:T(1024)S(1)}, f32[1536]{0:T(1024)}, u32[]{:S(2)}) copy-start(f32[1536]{0:T(1024)} %again.1) | copy-start | bytes 18436

commit v2 on v1

--- a/solution.py
+++ b/solution.py
@@ -15,18 +15,21 @@
 NEG = -1e30
 EPS = 1e-6
 MESH = pl.DeviceIdType.MESH
-LAG_Z = 1
-LAG_C = 2
+LAG_Z = 2
+LAG_C = 3
+WINDOW = 4
+AUDIO_PASS = 6
+AUDIO_READY = 7
 
 
 def kernel(
     n, heads, tok, aud, lmax,
     radius, tile_list, tile_count,
-    vq_hbm, vk_hbm, vv_hbm, aq_hbm, ak_hbm, av_hbm, vgain, again,
+    vq_hbm, vk_hbm, vv_hbm, aq_hbm, ak_hbm, av_hbm, vgain_hbm, again_hbm,
     vout, aout,
-    kv, audio, qown, aqown, aqin, qx, qr, part_o, part_s, back_o, back_s, attn, aattn,
-    load_sem, s_dk, r_dk, s_y, r_y, s_z, r_z, s_dy, r_dy, s_dz, r_dz,
-    s_aud, r_aud, s_daud, r_daud, s_q, r_q, s_bo, r_bo, s_bs, r_bs,
+    kv, audio, qown, aqown, aqin, qx, qr, part_o, part_s, back_o, back_s, attn, aattn, vgain, again,
+    load_sem, own_sem, s_dk, r_dk, s_y, r_y, s_z, r_z, s_dy, r_dy, s_dz, r_dz,
+    s_up, s_dn, s_ya, r_aud, s_daud, r_daud, s_q, r_q, s_bo, r_bo, s_bs, r_bs,
 ):
     me = lax.axis_index("seq")
     chips = n // 2
@@ -46,25 +49,54 @@
 
     barrier = pltpu.get_barrier_semaphore()
 
-    def greet(i, _):
-        pl.semaphore_signal(barrier, inc=1, device_id={"seq": (me + i) % n}, device_id_type=MESH)
-        return 0
-
-    lax.fori_loop(1, n, greet, 0)
+    def greet(device):
+        pl.semaphore_signal(barrier, inc=1, device_id={"seq": device}, device_id_type=MESH)
+
+    low, high = chip >= 2, chip + 2 < chips
+    greet(across)
+    greet(mate)
+    for exists, far_chip in ((high, chip + 2), (low, chip - 2)):
+        @pl.when(exists)
+        def _(far_chip=far_chip):
+            greet(jnp.clip(far_chip, 0, chips - 1) * 2)
+            greet(jnp.clip(far_chip, 0, chips - 1) * 2 + 1)
 
     loads = [
         pltpu.make_async_copy(aq_hbm, aqown, load_sem.at[0]),
         pltpu.make_async_copy(ak_hbm, audio.at[me, 0], load_sem.at[1]),
         pltpu.make_async_copy(av_hbm, audio.at[me, 1], load_sem.at[2]),
-        pltpu.make_async_copy(vk_hbm, kv.at[0, pl.ds(0, tok)], load_sem.at[3]),
-        pltpu.make_async_copy(vv_hbm, kv.at[1, pl.ds(0, tok)], load_sem.at[4]),
-        pltpu.make_async_copy(vq_hbm, qown, load_sem.at[5]),
+        pltpu.make_async_copy(vq_hbm, qown, load_sem.at[3]),
+        pltpu.make_async_copy(vgain_hbm, vgain, load_sem.at[4]),
+        pltpu.make_async_copy(again_hbm, again, load_sem.at[5]),
     ]
-    for load in loads:
+
+    def cols(h):
+        return pl.ds(pl.multiple_of(h * HD, HD), HD)
+
+    def own_head(h):
+        return [
+            pltpu.make_async_copy(side.at[:, cols(h)], kv.at[h, j, pl.ds(0, tok)], own_sem.at[h, j])
+            for j, side in enumerate((vk_hbm, vv_hbm))
+        ]
+
+    for load in loads[:3]:
+        load.start()
+
+    def load_own(h, _):
+        for load in own_head(h):
+            load.start()
+        return 0
+
+    lax.fori_loop(0, heads, load_own, 0)
+    for load in loads[3:]:
         load.start()
     @pl.when(jnp.logical_not(has_src))
     def _():
-        kv[:, pl.ds(4 * tok, 2 * tok), :] = jnp.zeros((2, 2 * tok, heads * HD), kv.dtype)
+        def clear(h, _):
+            kv[h, :, pl.ds(4 * tok, 2 * tok), :] = jnp.zeros((2, 2 * tok, HD), kv.dtype)
+            return 0
+
+        lax.fori_loop(0, heads, clear, 0)
 
     far = []
     for slot in range(4):
@@ -80,7 +112,7 @@
             back_o[slot] = jnp.zeros(back_o.shape[1:], back_o.dtype)
             back_s[slot] = jnp.zeros(back_s.shape[1:], back_s.dtype)
 
-    pl.semaphore_wait(barrier, n - 1)
+    pl.semaphore_wait(barrier, 2 + 2 * high.astype(jnp.int32) + 2 * low.astype(jnp.int32))
 
     def remote(src, dst, s, r, device):
         return pltpu.make_async_remote_copy(
@@ -101,26 +133,79 @@
     loads[1].wait()
     loads[2].wait()
 
-    def aud_copy(block, device, i):
-        return remote(audio.at[block], audio.at[block], s_aud.at[i], r_aud.at[block], device)
-
-    def daud_copy(block, i):
-        return remote(audio.at[block], audio.at[block], s_daud.at[i], r_daud.at[block], mate)
-
-    def send_audio(i, _):
-        aud_copy(me, (me + 2 * i) % n, i).start()
-        return 0
-
-    lax.fori_loop(1, chips, send_audio, 0)
-    daud_copy(me, 0).start()
-    loads[3].wait()
-    loads[4].wait()
-
-    def cols(h):
-        return pl.ds(pl.multiple_of(h * HD, HD), HD)
+    row, rows_all = chip // 2, chips // 2
+    up_to = jnp.clip(chip + 2, 0, chips - 1) * 2 + core
+    down_to = jnp.clip(chip - 2, 0, chips - 1) * 2 + core
+
+    def aud_copy(sems, block, device):
+        return remote(audio.at[block], audio.at[block], sems.at[block], r_aud.at[block], device)
+
+    def daud_copy(block):
+        return remote(audio.at[block], audio.at[block], s_daud.at[block], r_daud.at[block], mate)
+
+    def spread_up(block):
+        return aud_copy(s_up, block, up_to)
+
+    def spread_down(block):
+        return aud_copy(s_dn, block, down_to)
+
+    def spread_across(block):
+        return aud_copy(s_ya, block, across)
+
+    def from_below(d, act):
+        @pl.when(row - d >= 0)
+        def _():
+            block = jnp.maximum(me - 4 * d, 0)
+            act(block)
+
+    def from_above(d, act):
+        @pl.when(row + d < rows_all)
+        def _():
+            block = jnp.minimum(me + 4 * d, n - 1)
+            act(block)
+
+    @pl.when(high)
+    def _():
+        spread_up(me).start()
+
+    @pl.when(low)
+    def _():
+        spread_down(me).start()
+
+    def column_step(d):
+        def below(block):
+            spread_up(block).wait_recv()
+
+            @pl.when(high)
+            def _():
+                spread_up(block).start()
+            spread_across(block).start()
+            daud_copy(block).start()
+
+        def above(block):
+            spread_down(block).wait_recv()
+
+            @pl.when(low)
+            def _():
+                spread_down(block).start()
+            spread_across(block).start()
+            daud_copy(block).start()
+
+        from_below(d, below)
+        from_above(d, above)
+
+    def pass_audio(i, _):
+        block = 4 * i + across % 4
+        spread_across(block).wait_recv()
+        daud_copy(block).start()
+        return 0
+
+    def take_audio(i, _):
+        daud_copy(2 * i + 1 - core).wait_recv()
+        return 0
 
     def kv_head(slot, h):
-        return kv.at[:, pl.ds(slot * tok, tok), cols(h)]
+        return kv.at[h, :, pl.ds(slot * tok, tok)]
 
     def y_copy(h):
         return remote(kv_head(0, h), kv_head(2, h), s_y.at[h], r_y.at[h], across)
@@ -134,39 +219,38 @@
     def dz_copy(h):
         return remote(kv_head(4, h), kv_head(5, h), s_dz.at[h], r_dz.at[h], mate)
 
-    dk = remote(kv.at[:, pl.ds(0, tok)], kv.at[:, pl.ds(tok, tok)], s_dk, r_dk, mate)
-
-    def send_y(h, _):
+    dk = remote(kv.at[:, :, pl.ds(0, tok)], kv.at[:, :, pl.ds(tok, tok)], s_dk, r_dk, mate)
+
+    def own_there(h, _):
+        for load in own_head(h):
+            load.wait()
+        return 0
+
+    for h in range(2):
+        own_there(h, 0)
         y_copy(h).start()
-        return 0
-
-    lax.fori_loop(0, heads, send_y, 0)
+    spread_across(me).start()
+    daud_copy(me).start()
+    lax.fori_loop(2, heads, own_there, 0)
+    for h in range(2, WINDOW):
+        y_copy(h).start()
     dk.start()
 
-    loads[5].wait()
+    loads[3].wait()
     wide = jnp.concatenate([aqown[...].astype(jnp.float32), jnp.zeros((aud, heads * HD), jnp.float32)], axis=0)
     qx[...] = wide.astype(jnp.bfloat16)
 
-    for slot, exists, device, there in far:
-        @pl.when(exists)
-        def _(slot=slot):
-            q_arrival(slot).wait_recv()
-    for pair in range(2):
-        both = jnp.concatenate(
-            [aqin[2 * pair].astype(jnp.float32), aqin[2 * pair + 1].astype(jnp.float32)], axis=0)
-        qr[pl.ds(2 * aud * pair, 2 * aud), :] = both.astype(jnp.bfloat16)
-    lane = lax.broadcasted_iota(jnp.int32, (4 * aud, HD), 1)
-    part_s[...] = jnp.zeros(part_s.shape, jnp.float32)
-
     def dot_t(a, b):
         return lax.dot_general(a, b, (((1,), (1,)), ((), ())), preferred_element_type=jnp.float32)
 
+    lane = lax.broadcasted_iota(jnp.int32, (4 * aud, HD), 1)
+
     def far_head(h, _):
-        s = dot_t(qr[:, cols(h)], kv[0, pl.ds(0, tok), cols(h)]) * SCALE
+        s = dot_t(qr[:, cols(h)], kv[h, 0, pl.ds(0, tok)]) * SCALE
         m = jnp.max(s, axis=1, keepdims=True)
         w = jnp.exp2(s - m).astype(jnp.bfloat16)
         total = jnp.sum(w.astype(jnp.float32), axis=1, keepdims=True)
-        o = jnp.dot(w, kv[1, pl.ds(0, tok), cols(h)], preferred_element_type=jnp.float32) / total
+        o = jnp.dot(w, kv[h, 1, pl.ds(0, tok)], preferred_element_type=jnp.float32) / total
         for slot in range(4):
             rows = slice(slot * aud, (slot + 1) * aud)
             part_o[slot, :, cols(h)] = o[rows].astype(part_o.dtype)
@@ -176,49 +260,37 @@
             part_s[slot] = st
         return 0
 
-    lax.fori_loop(0, heads, far_head, 0)
-
     def bo_copy(slot, device, there):
         return remote(part_o.at[slot], back_o.at[there], s_bo.at[slot], r_bo.at[there], device)
 
     def bs_copy(slot, device, there):
         return remote(part_s.at[slot], back_s.at[there], s_bs.at[slot], r_bs.at[there], device)
 
-    for slot, exists, device, there in far:
-        @pl.when(exists)
-        def _(slot=slot, device=device, there=there):
-            bo_copy(slot, device, there).start()
-            bs_copy(slot, device, there).start()
-
-    def pass_audio(i, _):
-        block = (me + 2 * i) % n
-        aud_copy(block, mate, i).wait_recv()
-        daud_copy(block, i).start()
-        return 0
-
-    lax.fori_loop(1, chips, pass_audio, 0)
-
-    def take_audio(i, _):
-        daud_copy((mate + 2 * i) % n, i).wait_recv()
-        return 0
-
-    lax.fori_loop(0, chips, take_audio, 0)
+    def far_part():
+        for slot, exists, device, there in far:
+            @pl.when(exists)
+            def _(slot=slot):
+                q_arrival(slot).wait_recv()
+        for pair in range(2):
+            both = jnp.concatenate(
+                [aqin[2 * pair].astype(jnp.float32), aqin[2 * pair + 1].astype(jnp.float32)], axis=0)
+            qr[pl.ds(2 * aud * pair, 2 * aud), :] = both.astype(jnp.bfloat16)
+        part_s[...] = jnp.zeros(part_s.shape, jnp.float32)
+        lax.fori_loop(0, heads, far_head, 0)
+        for slot, exists, device, there in far:
+            @pl.when(exists)
+            def _(slot=slot, device=device, there=there):
+                bo_copy(slot, device, there).start()
+                bs_copy(slot, device, there).start()
 
     def lay_audio(i, _):
         for j in range(2):
             pair = jnp.concatenate(
                 [audio[2 * i, j].astype(jnp.float32), audio[2 * i + 1, j].astype(jnp.float32)], axis=0)
-            kv[j, pl.ds(pl.multiple_of(6 * tok + 2 * aud * i, 2 * aud), 2 * aud), :] = pair.astype(jnp.bfloat16)
-        return 0
-
-    lax.fori_loop(0, chips, lay_audio, 0)
-
-    for slot, exists, device, there in far:
-        @pl.when(exists)
-        def _(slot=slot):
-            bo_copy(slot, mate, slot).wait_recv()
-            bs_copy(slot, mate, slot).wait_recv()
-    dk.wait_recv()
+            pair = pair.astype(jnp.bfloat16)
+            for h in range(heads):
+                kv[h, j, pl.ds(pl.multiple_of(6 * tok + 2 * aud * i, 2 * aud), 2 * aud), :] = pair[:, h * HD:(h + 1) * HD]
+        return 0
 
     near = radius[0]
     count = tile_count[me]
@@ -226,7 +298,7 @@
     def is_listed(tile):
         listed = jnp.int32(0)
         for j in range(lmax):
-            listed = jnp.where((tile_list[me, j] == tile) & (j < count), 1, listed)
+            listed = jnp.where((tile_list[j, me] == tile) & (j < count), 1, listed)
         return listed > 0
 
     tiles = [me, mate, across, across_chip * 2 + 1 - core, zchip * 2 + core, zchip * 2 + 1 - core]
@@ -255,12 +327,12 @@
 
     def head(h):
         q = jnp.concatenate([qown[:, cols(h)], qx[:, cols(h)]], axis=0)
-        s = dot_t(q, kv[0, :, cols(h)])
+        s = dot_t(q, kv[h, 0])
         _, wv = softmax_part(s[:tok], see_v)
         ma, wa = softmax_part(s[tok:, :span], see_a)
         wa = jnp.concatenate([wa, jnp.zeros((2 * aud, keys - span), jnp.bfloat16)], axis=1)
         w = jnp.concatenate([wv, wa], axis=0)
-        v = kv[1, :, cols(h)]
+        v = kv[h, 1]
         o = jnp.dot(w, jnp.concatenate([v, jnp.ones((keys, HD), jnp.bfloat16)], axis=1), preferred_element_type=jnp.float32)
         attn[:, cols(h)] = o[:tok, :HD] / o[:tok, HD:]
         oa = o[tok:tok + aud, :HD]
@@ -289,6 +361,10 @@
             @pl.when(has_fwd)
             def _():
                 z_copy(i).start()
+
+            @pl.when(i + WINDOW < heads)
+            def _():
+                y_copy(i + WINDOW).start()
             dy_copy(i).start()
 
         @pl.when((i >= LAG_Z) & (i < heads + LAG_Z) & has_src)
@@ -296,16 +372,53 @@
             z_copy(i - LAG_Z).wait_recv()
             dz_copy(i - LAG_Z).start()
 
-        @pl.when(i >= LAG_C)
-        def _():
-            h = i - LAG_C
+        @pl.when(i == 0)
+        def _():
+            column_step(1)
+
+        @pl.when(i == 1)
+        def _():
+            far_part()
+            if rows_all > 2:
+                column_step(2)
+
+        @pl.when(i == 2)
+        def _():
+            def more(d, _):
+                column_step(d)
+                return 0
+
+            lax.fori_loop(3, rows_all, more, 0)
+
+        @pl.when(i == AUDIO_PASS)
+        def _():
+            lax.fori_loop(0, rows_all, pass_audio, 0)
+
+        @pl.when(i == AUDIO_READY)
+        def _():
+            lax.fori_loop(0, chips, take_audio, 0)
+            lax.fori_loop(0, chips, lay_audio, 0)
+            for slot, exists, device, there in far:
+                @pl.when(exists)
+                def _(slot=slot):
+                    bo_copy(slot, mate, slot).wait_recv()
+                    bs_copy(slot, mate, slot).wait_recv()
+            dk.wait_recv()
+
+        def attend(h, _):
             dy_copy(h).wait_recv()
 
             @pl.when(has_src)
             def _():
                 dz_copy(h).wait_recv()
             head(h)
-        return 0
+            return 0
+
+        lax.fori_loop(done(i - 1), done(i), attend, 0)
+        return 0
+
+    def done(i):
+        return jnp.clip(jnp.minimum(2 * (i - AUDIO_READY + 1), i - LAG_C + 1), 0, heads)
 
     lax.fori_loop(0, heads + LAG_C, relay, 0)
 
@@ -313,6 +426,8 @@
         scale = lax.rsqrt(jnp.mean(mixed * mixed, axis=1, keepdims=True) + EPS)
         return (mixed * scale * gain).astype(jnp.bfloat16)
 
+    loads[4].wait()
+    loads[5].wait()
     vout[...] = finish(attn[...], vgain[...].reshape(1, heads * HD))
     aout[...] = finish(aattn[...], again[...].reshape(1, heads * HD))
 
@@ -323,14 +438,36 @@
             bo_copy(slot, device, there).wait_send()
             bs_copy(slot, device, there).wait_send()
 
-    def audio_left(i, _):
-        aud_copy(me, mate, i).wait_send()
-        return 0
-
-    lax.fori_loop(1, chips, audio_left, 0)
+    @pl.when(high)
+    def _():
+        spread_up(me).wait_send()
+
+    @pl.when(low)
+    def _():
+        spread_down(me).wait_send()
+    spread_across(me).wait_send()
+
+    def column_left(d, _):
+        def below(block):
+            @pl.when(high)
+            def _():
+                spread_up(block).wait_send()
+            spread_across(block).wait_send()
+
+        def above(block):
+            @pl.when(low)
+            def _():
+                spread_down(block).wait_send()
+            spread_across(block).wait_send()
+
+        from_below(d, below)
+        from_above(d, above)
+        return 0
+
+    lax.fori_loop(1, rows_all, column_left, 0)
 
     def daudio_left(i, _):
-        daud_copy(me, i).wait_send()
+        daud_copy(2 * i + core).wait_send()
         return 0
 
     lax.fori_loop(0, chips, daudio_left, 0)
@@ -365,15 +502,15 @@
         dma = pltpu.SemaphoreType.DMA
         per_head = dma((heads,))
         smem = pl.BlockSpec(memory_space=pltpu.SMEM)
-        anyw = pl.BlockSpec(memory_space=pl.ANY)
+        hbm = pl.BlockSpec(memory_space=pltpu.HBM)
         vmem = pl.BlockSpec(memory_space=pltpu.VMEM)
         return pl.pallas_call(
             functools.partial(kernel, n, heads, tok, aud, tile_list.shape[1]),
             out_shape=(jax.ShapeDtypeStruct(vq.shape, bf), jax.ShapeDtypeStruct(aq.shape, bf)),
-            in_specs=[smem] * 3 + [anyw] * 6 + [vmem] * 2,
+            in_specs=[smem] * 3 + [hbm] * 8,
             out_specs=(vmem, vmem),
             scratch_shapes=[
-                pltpu.VMEM((2, keys, width), bf),
+                pltpu.VMEM((heads, 2, keys, HD), bf),
                 pltpu.VMEM((n, 2, aud, width), bf),
                 pltpu.VMEM((tok, width), bf),
                 pltpu.VMEM((aud, width), bf),
@@ -386,14 +523,16 @@
                 pltpu.VMEM((4, aud, HD), f32),
                 pltpu.VMEM((tok, width), f32),
                 pltpu.VMEM((aud, width), f32),
-                dma((6,)), dma, dma,
+                pltpu.VMEM((width,), f32),
+                pltpu.VMEM((width,), f32),
+                dma((6,)), dma((heads, 2)), dma, dma,
                 *([per_head] * 8),
-                dma((chips,)), dma((n,)), dma((chips,)), dma((n,)),
+                *([dma((n,))] * 6),
                 *([dma((4,))] * 6),
             ],
             compiler_params=pltpu.CompilerParams(
-                collective_id=0, has_side_effects=True, vmem_limit_bytes=48 * 1024 * 1024),
-        )(radius, tile_list, tile_count, vq, vk, vv, aq, ak, av, vgain, again)
+                collective_id=0, has_side_effects=True),
+        )(radius, tile_list.T, tile_count, vq, vk, vv, aq, ak, av, vgain, again)
 
     rows = P(("clips", "seq"), None)
     return jax.shard_map(

time: 53.7 us -> 41.8 us (0.78)
  Pallas kernels: 43.8 us -> 37.9 us
  local copies, waits for them, and re-layouts: 8.03 us -> 2.38 us
    pallas_call x1, Pallas kernels: 43.8 us -> 37.9 us  [on_device(): pl.pallas_call(functools.partial(kernel, n, heads, tok, aud, tile_list.sh...]
    unnamed x21 -> x4, local copies, waits for them, and re-layouts: 8.03 us -> 2.38 us
where the time goes in v2:
time: 41.8 us; the launch traced here: 41.6 us
  Pallas kernels  37.9 us (91%)
  local copies, waits for them, and re-layouts  2.38 us (6%)
  between operations  1.3 us (3%)
    pallas_call x1, Pallas kernels, on_device(): pl.pallas_call(functools.partial(kernel, n, heads, tok, aud, tile_list.sh...  37.9 us
    unnamed x4, local copies, waits for them, and re-layouts  2.38 us

profile of v2, /device:TPU:5, one launch (start us, length us, event | category | flops | bytes accessed | tf_op | source)
XLA Modules:
  0.0 41.6 jit_solution(10046973037380102350)
XLA Ops:
  1.3 37.9 %shard_map.122 = (bf16[128,1536]{1,0:T(8,128)(2,1)}, bf16[8,1536]{1,0:T(8,128)(2,1)}) custom-call(s32[1]{0:T(128)S(6)} %copy.15.radius, s32[5,16]{1,0:T(8,128)} %bitcast.1, s32[16]{0:T(128)} %tile_count.1, bf16[128,1536]{1,0:T(8,128)(2,1)} %vq_hbm.1, bf16[128,1536]{1,0:T(8,128)(2,1)} %vk_hbm.1, bf16[128,1536]{1,0:T(8,128)(2,1)} %vv_hbm.1, ...), custom_call_target="tpu_custom_call" | custom-call | tf_op jit(solution)/shard_map/pallas_call | solution.py:507
  39.2 0.0 copy-start
  39.2 1.8 %copy.16 = bf16[128,1536]{1,0:T(8,128)(2,1)} copy(bf16[128,1536]{1,0:T(8,128)(2,1)} %get-tuple-element.4) | data formatting | bytes 786432
  41.0 0.0 copy-done
  41.0 0.6 %copy.17 = bf16[8,1536]{1,0:T(8,128)(2,1)} copy(bf16[8,1536]{1,0:T(8,128)(2,1)S(1)} %copy-done) | data formatting | bytes 49152
Async XLA Ops:
  39.2 1.8 %copy-start = (bf16[8,1536]{1,0:T(8,128)(2,1)S(1)}, bf16[8,1536]{1,0:T(8,128)(2,1)}, u32[]{:S(2)}) copy-start(bf16[8,1536]{1,0:T(8,128)(2,1)} %get-tuple-element.5) | copy-start | bytes 73732
